TPU v7x, 32 devices: a whole 2x2x4 slice. The times are simulated.
32 devices in a mesh: gx: 8 (over z, y), gy: 4 (over x, core).
Axes of the slice: x: 2, y: 2, z: 4, core: 2. Of those that a mesh axis runs over, the one named last changes fastest.
Arguments:
- ice_rhs: float32 [2, 512, 1024], P(None, 'gx', 'gy'), may hold values from -18.6 to 18.6
- ice_guess: float32 [2, 512, 1024], P(None, 'gx', 'gy'), may hold values from -9.3 to 9.3
- ocean_rhs: float32 [512, 1024], P('gx', 'gy'), may hold values from -18.6 to 18.6
- ocean_guess: float32 [512, 1024], P('gx', 'gy'), may hold values from -9.3 to 9.3
- ice_diag: float32 [512, 1024], P('gx', 'gy'), may hold values from 1 to 4
- ice_visc: float32 [512, 1024], P('gx', 'gy'), may hold values from 0.5 to 1.5
- coriolis: float32 [512, 1024], P('gx', 'gy'), may hold values from -1.5 to 1.5
- depth_factor: float32 [512, 1024], P('gx', 'gy'), may hold values from 1 to 3
- wet_mask: int32 [512, 1024], P('gx', 'gy'), may hold values 0 or 1
- ice_mask: int32 [512, 1024], P('gx', 'gy'), may hold values from 0 to 1, as said below
Outputs:
- ice_velocity: float32 [2, 512, 1024], P(None, 'gx', 'gy')
- ocean_level: float32 [512, 1024], P('gx', 'gy')
Inputs may be any that keep to these rules, and one draw needn't show every extreme that they name: `ice_mask`: 1 where sea ice covers the cell.
All inputs are finite; a program needn't handle non-finite values. No bound on the sum of `wet_mask` on one device may be relied on, other than what follows from the above.
Results may differ from a plain program's by a relative error of at most 0.00005.
Values sent between devices are 32-bit elements; how exact they have to be, the bound alone decides.
A program may use at most 64 MiB of HBM per device.

v0:
```python
import jax
import jax.numpy as jnp
from jax import lax
from jax.sharding import PartitionSpec as P


def shifted(value, axis, by):
    size = lax.axis_size(axis)
    pairs = [(i, i + by) for i in range(size) if 0 <= i + by < size]
    return lax.ppermute(value, axis, pairs)


def extended(cells, sides, width, closed):
    for axis, dim in sides:
        count = lax.axis_size(axis)
        ends = count if closed else count - 1
        head = lax.slice_in_dim(cells, 0, width, axis=dim)
        tail = lax.slice_in_dim(cells, cells.shape[dim] - width, cells.shape[dim], axis=dim)
        cells = jnp.concatenate(
            [
                lax.ppermute(tail, axis, [(i, (i + 1) % count) for i in range(ends)]),
                cells,
                lax.ppermute(head, axis, [((i + 1) % count, i) for i in range(ends)]),
            ],
            axis=dim,
        )
    return cells


def inner(left, right):
    return jnp.sum(left * right)


def body(
    ice_rhs,
    ice_guess,
    ocean_rhs,
    ocean_guess,
    ice_diag,
    ice_visc,
    coriolis,
    depth_factor,
    wet_mask,
    ice_mask,
):
    wet = wet_mask.astype(jnp.float32)
    active = wet * ice_mask.astype(jnp.float32)
    act = jnp.stack([active, active, wet])
    root = jnp.stack([ice_visc, ice_visc, depth_factor])
    diag = jnp.stack([ice_diag, ice_diag, jnp.ones_like(ice_diag)])
    inverse = 1.0 / (act * (diag + 4.0 * root * root) + 1.0 - act)
    signs = jnp.array([-1.0, -1.0, 1.0], jnp.float32)[:, None]
    at_top = lax.axis_index("gy") == lax.axis_size("gy") - 1

    def mirror_sections():
        sections = []
        group = lax.axis_size("gx")
        while group % 2 == 0:
            sections.append((group // 2, group, 0))
            group = group // 2
        for offset in range(2, group, 2):
            sections.append((offset, group, 1))
        return sections

    def partner_row(q):
        moving = q[:, :, -1]
        position = lax.axis_index("gx")
        for distance, extent, sort_kind in mirror_sections():
            within = position % extent
            from_above = shifted(moving, "gx", -distance)
            from_below = shifted(moving, "gx", distance)
            if sort_kind == 0:
                take_above = within < distance
                take_below = within >= distance
            else:
                take_above = extent - 1 - 2 * within == distance
                take_below = extent - 1 - 2 * within == -distance
            moving = jnp.where(take_above, from_above, jnp.where(take_below, from_below, moving))
        return moving[:, ::-1]

    def operate(field):
        q = act * root * field
        zonal = extended(q, (("gx", 1),), 1, True)
        merid = extended(q, (("gy", 2),), 1, False)
        ghost = jnp.where(at_top, signs * partner_row(q), 0.0)
        north = jnp.concatenate([merid[:, :, 2:-1], merid[:, :, -1:] + ghost[:, :, None]], axis=2)
        beside_all = zonal[:, 2:, :] + zonal[:, :-2, :] + north + merid[:, :, :-2]
        lap = 4.0 * q - beside_all
        turn = jnp.stack([-coriolis * field[1], coriolis * field[0], jnp.zeros_like(coriolis)])
        return act * (diag * field + root * lap + turn) + (1.0 - act) * field

    start_image = operate(jnp.concatenate([ice_guess, ocean_guess[None]]))
    resid = jnp.concatenate([ice_rhs, ocean_rhs[None]]) - start_image
    r = resid[:2]
    ro = resid[2]
    pre = inverse * resid
    image = operate(pre)
    w_scaled = image[:2]
    az0 = image[2]
    z_scaled = pre[:2]
    z0 = pre[2]

    def merged(values):
        return lax.psum(jnp.stack(values), ("gx", "gy"))

    sums = merged(
        [inner(r, r), inner(w_scaled, r), inner(w_scaled, w_scaled), inner(ro, z0), inner(z0, az0)]
    )
    rr = sums[0]
    beta = jnp.sqrt(rr)
    h11 = sums[1] / rr
    g11 = sums[2] / rr
    h21 = jnp.sqrt(g11 - h11 * h11)
    gamma0 = sums[3]
    alpha0 = gamma0 / sums[4]
    v2 = (w_scaled - h11 * r) / (beta * h21)
    level = ocean_guess + alpha0 * z0
    ro = ro - alpha0 * az0
    znext = inverse[2] * ro
    image2 = operate(jnp.concatenate([inverse[:2] * v2, znext[None]]))
    w2 = image2[:2]
    sums = merged(
        [inner(w2, r), inner(w2, v2), inner(w2, w2), inner(ro, znext), inner(znext, image2[2])]
    )
    h12 = sums[0] / beta
    h22 = sums[1]
    g22 = sums[2]
    gamma1 = sums[3]
    lead = gamma1 / gamma0
    alpha1 = gamma1 / (sums[4] - lead * gamma1 / alpha0)
    p1 = znext + lead * z0
    level = level + alpha1 * p1
    g12 = h11 * h12 + h21 * h22
    first_rhs = beta * h11
    second_rhs = beta * h12
    det = g11 * g22 - g12 * g12
    y_first = (g22 * first_rhs - g12 * second_rhs) / det
    y_second = (g11 * second_rhs - g12 * first_rhs) / det
    velocity = ice_guess + y_first * (z_scaled / beta) + y_second * (inverse[:2] * v2)
    return (velocity, level)


def solution(mesh):
    placed = (
        P(None, "gx", "gy"),
        P(None, "gx", "gy"),
        P("gx", "gy"),
        P("gx", "gy"),
        P("gx", "gy"),
        P("gx", "gy"),
        P("gx", "gy"),
        P("gx", "gy"),
        P("gx", "gy"),
        P("gx", "gy"),
    )
    return jax.shard_map(
        body,
        mesh=mesh,
        in_specs=placed,
        out_specs=(P(None, "gx", "gy"), P("gx", "gy")),
        check_vma=False,
    )
```

profile of v0, /device:TPU:0, one launch (start us, length us, event | category | flops | bytes accessed | tf_op | source)
XLA Modules:
  0.0 202.8 jit_solution(5238889771545232781)
XLA Ops:
  4.0 6.0 %collective-permute-start.4 = (f32[3,64]{1,0:T(4,128)S(1)}, f32[3,64]{1,0:T(4,128)S(1)}, u32[]{:S(2)}, u32[]{:S(2)}) collective-permute-start(f32[3,64]{1,0:T(4,128)S(1)} %get-tuple-element.39), channel_id=1, source_target_pairs={{0,16},{4,20},{8,24},{12,28},{1,17},{5,21},{9,25},{13,29},{2,18},{... | collective-permute-start | bytes 2312 | tf_op jit(solution)/shard_map/ppermute | solution.py:10
  11.3 3.0 %collective-permute-start.9 = (f32[3,64,1]{2,1,0:T(8,128)S(1)}, f32[3,64,1]{2,1,0:T(8,128)S(1)}, u32[]{:S(2)}, u32[]{:S(2)}) collective-permute-start(f32[3,64,1]{2,1,0:T(8,128)S(1)} %get-tuple-element.40), channel_id=1, source_target_pairs={{0,1},{1,2},{2,3},{4,5},{5,6},{6,7},{8,9},{9,10},{10,11},{12,13},{... | collective-permute-start | bytes 2312 | tf_op jit(solution)/shard_map/ppermute | solution.py:21
  14.4 2.4 %collective-permute-start = (f32[3,1,256]{2,1,0:T(1,128)S(1)}, f32[3,1,256]{2,1,0:T(1,128)S(1)}, u32[]{:S(2)}, u32[]{:S(2)}) collective-permute-start(f32[3,1,256]{2,1,0:T(1,128)S(1)} %get-tuple-element.37), channel_id=1, source_target_pairs={{4,0},{8,4},{12,8},{16,12},{20,16},{24,20},{28,24},{0,28},{5,1},{9... | collective-permute-start | bytes 9224 | tf_op jit(solution)/shard_map/ppermute | solution.py:23
  18.1 4.5 %collective-permute-start.6 = (f32[3,64]{1,0:T(4,128)S(1)}, f32[3,64]{1,0:T(4,128)S(1)}, u32[]{:S(2)}, u32[]{:S(2)}) collective-permute-start(f32[3,64]{1,0:T(4,128)S(1)} %select_select_fusion.8), channel_id=1, source_target_pairs={{0,8},{4,12},{8,16},{12,20},{16,24},{20,28},{1,9},{5,13},{9,17},{1... | collective-permute-start | bytes 2312 | tf_op jit(solution)/shard_map/ppermute | solution.py:10
  25.2 4.5 %collective-permute-start.8 = (f32[3,64]{1,0:T(4,128)S(1)}, f32[3,64]{1,0:T(4,128)S(1)}, u32[]{:S(2)}, u32[]{:S(2)}) collective-permute-start(f32[3,64]{1,0:T(4,128)S(1)} %select_select_fusion.7), channel_id=1, source_target_pairs={{0,4},{4,8},{8,12},{12,16},{16,20},{20,24},{24,28},{1,5},{5,9},{9,... | collective-permute-start | bytes 2312 | tf_op jit(solution)/shard_map/ppermute | solution.py:10
  30.1 1.7 collective-permute-start.1
  32.7 3.6 %collective-permute-done.1 = f32[3,1,256]{2,1,0:T(1,128)S(1)} collective-permute-done((f32[3,1,256]{2,1,0:T(1,128)S(1)}, f32[3,1,256]{2,1,0:T(1,128)S(1)}, u32[]{:S(2)}, u32[]{:S(2)}) %collective-permute-start.1) | collective-permute-done | bytes 3104 | tf_op jit(solution)/shard_map/ppermute | solution.py:21
  38.1 5.4 %collective-permute-start.14 = (f32[3,64]{1,0:T(4,128)S(1)}, f32[3,64]{1,0:T(4,128)S(1)}, u32[]{:S(2)}, u32[]{:S(2)}) collective-permute-start(f32[3,64]{1,0:T(4,128)S(1)} %get-tuple-element.32), channel_id=1, source_target_pairs={{0,16},{4,20},{8,24},{12,28},{1,17},{5,21},{9,25},{13,29},{2,18},{... | collective-permute-start | bytes 2312 | tf_op jit(solution)/shard_map/ppermute | solution.py:10
  43.6 1.3 collective-permute-start.19
  46.2 4.5 %collective-permute-start.16 = (f32[3,64]{1,0:T(4,128)S(1)}, f32[3,64]{1,0:T(4,128)S(1)}, u32[]{:S(2)}, u32[]{:S(2)}) collective-permute-start(f32[3,64]{1,0:T(4,128)S(1)} %select_select_fusion.5), channel_id=1, source_target_pairs={{0,8},{4,12},{8,16},{12,20},{16,24},{20,28},{1,9},{5,13},{9,17},{1... | collective-permute-start | bytes 2312 | tf_op jit(solution)/shard_map/ppermute | solution.py:10
  53.5 4.5 %collective-permute-start.18 = (f32[3,64]{1,0:T(4,128)S(1)}, f32[3,64]{1,0:T(4,128)S(1)}, u32[]{:S(2)}, u32[]{:S(2)}) collective-permute-start(f32[3,64]{1,0:T(4,128)S(1)} %select_select_fusion.4), channel_id=1, source_target_pairs={{0,4},{4,8},{8,12},{12,16},{16,20},{20,24},{24,28},{1,5},{5,9},{9,... | collective-permute-start | bytes 2312 | tf_op jit(solution)/shard_map/ppermute | solution.py:10
  58.1 3.5 %collective-permute-start.10 = (f32[3,1,256]{2,1,0:T(1,128)S(1)}, f32[3,1,256]{2,1,0:T(1,128)S(1)}, u32[]{:S(2)}, u32[]{:S(2)}) collective-permute-start(f32[3,1,256]{2,1,0:T(1,128)S(1)} %get-tuple-element.35), channel_id=1, source_target_pairs={{4,0},{8,4},{12,8},{16,12},{20,16},{24,20},{28,24},{0,28},{5,1},{9... | collective-permute-start | bytes 9224 | tf_op jit(solution)/shard_map/ppermute | solution.py:23
  62.9 5.0 %collective-permute-done.11 = f32[3,1,256]{2,1,0:T(1,128)S(1)} collective-permute-done((f32[3,1,256]{2,1,0:T(1,128)S(1)}, f32[3,1,256]{2,1,0:T(1,128)S(1)}, u32[]{:S(2)}, u32[]{:S(2)}) %collective-permute-start.11) | collective-permute-done | bytes 3104 | tf_op jit(solution)/shard_map/ppermute | solution.py:21
  69.5 3.3 %stack.109 = f32[5]{0:T(128)S(1)} concatenate(f32[1]{0:T(128)} %bitcast.17, f32[1]{0:T(128)} %bitcast.18, f32[1]{0:T(128)} %bitcast.19, f32[1]{0:T(128)} %bitcast.22, f32[1]{0:T(128)} %bitcast.24), dimensions={0} | concatenate | bytes 40 | tf_op jit(solution)/shard_map/stack | solution.py:104
  72.7 36.8 %psum.14 = f32[5]{0:T(128)S(1)} all-reduce(f32[5]{0:T(128)S(1)} %stack.109), channel_id=1, replica_groups=mesh['gx'=8,'gy'=4] {'gx','gy'}, use_global_device_ids=true, to_apply=%region_5.6 | all-reduce | flops 5 | bytes 40 | tf_op jit(solution)/shard_map/psum | solution.py:104
  116.3 5.4 %collective-permute-start.24 = (f32[3,64]{1,0:T(4,128)S(1)}, f32[3,64]{1,0:T(4,128)S(1)}, u32[]{:S(2)}, u32[]{:S(2)}) collective-permute-start(f32[3,64]{1,0:T(4,128)S(1)} %get-tuple-element.27), channel_id=1, source_target_pairs={{0,16},{4,20},{8,24},{12,28},{1,17},{5,21},{9,25},{13,29},{2,18},{... | collective-permute-start | bytes 2312 | tf_op jit(solution)/shard_map/ppermute | solution.py:10
  124.3 5.4 %collective-permute-start.26 = (f32[3,64]{1,0:T(4,128)S(1)}, f32[3,64]{1,0:T(4,128)S(1)}, u32[]{:S(2)}, u32[]{:S(2)}) collective-permute-start(f32[3,64]{1,0:T(4,128)S(1)} %select_select_fusion.2), channel_id=1, source_target_pairs={{0,8},{4,12},{8,16},{12,20},{16,24},{20,28},{1,9},{5,13},{9,17},{1... | collective-permute-start | bytes 2312 | tf_op jit(solution)/shard_map/ppermute | solution.py:10
  132.3 4.8 %collective-permute-start.28 = (f32[3,64]{1,0:T(4,128)S(1)}, f32[3,64]{1,0:T(4,128)S(1)}, u32[]{:S(2)}, u32[]{:S(2)}) collective-permute-start(f32[3,64]{1,0:T(4,128)S(1)} %select_select_fusion.1), channel_id=1, source_target_pairs={{0,4},{4,8},{8,12},{12,16},{16,20},{20,24},{24,28},{1,5},{5,9},{9,... | collective-permute-start | bytes 2312 | tf_op jit(solution)/shard_map/ppermute | solution.py:10
  137.3 1.3 collective-permute-start.22
  138.6 3.0 %collective-permute-start.29 = (f32[3,64,1]{2,1,0:T(8,128)S(1)}, f32[3,64,1]{2,1,0:T(8,128)S(1)}, u32[]{:S(2)}, u32[]{:S(2)}) collective-permute-start(f32[3,64,1]{2,1,0:T(8,128)S(1)} %get-tuple-element.28), channel_id=1, source_target_pairs={{0,1},{1,2},{2,3},{4,5},{5,6},{6,7},{8,9},{9,10},{10,11},{12,13},{... | collective-permute-start | bytes 2312 | tf_op jit(solution)/shard_map/ppermute | solution.py:21
  141.6 2.9 %collective-permute-start.20 = (f32[3,1,256]{2,1,0:T(1,128)S(1)}, f32[3,1,256]{2,1,0:T(1,128)S(1)}, u32[]{:S(2)}, u32[]{:S(2)}) collective-permute-start(f32[3,1,256]{2,1,0:T(1,128)S(1)} %get-tuple-element.30), channel_id=1, source_target_pairs={{4,0},{8,4},{12,8},{16,12},{20,16},{24,20},{28,24},{0,28},{5,1},{9... | collective-permute-start | bytes 9224 | tf_op jit(solution)/shard_map/ppermute | solution.py:23
  146.2 4.6 %collective-permute-done.21 = f32[3,1,256]{2,1,0:T(1,128)S(1)} collective-permute-done((f32[3,1,256]{2,1,0:T(1,128)S(1)}, f32[3,1,256]{2,1,0:T(1,128)S(1)}, u32[]{:S(2)}, u32[]{:S(2)}) %collective-permute-start.21) | collective-permute-done | bytes 3104 | tf_op jit(solution)/shard_map/ppermute | solution.py:21
  152.3 3.1 %stack.118 = f32[5]{0:T(128)S(1)} concatenate(f32[1]{0:T(128)} %bitcast.35, f32[1]{0:T(128)} %bitcast.36, f32[1]{0:T(128)} %bitcast.37, f32[1]{0:T(128)} %bitcast.39, f32[1]{0:T(128)} %bitcast.41), dimensions={0} | concatenate | bytes 40 | tf_op jit(solution)/shard_map/stack | solution.py:104
  155.4 38.4 %psum.15 = f32[5]{0:T(128)S(1)} all-reduce(f32[5]{0:T(128)S(1)} %stack.118), channel_id=1, replica_groups=mesh['gx'=8,'gy'=4] {'gx','gy'}, use_global_device_ids=true, to_apply=%region_11.12 | all-reduce | flops 5 | bytes 40 | tf_op jit(solution)/shard_map/psum | solution.py:104
  (110 shorter events, 30.8 us)
Async XLA Ops:
  2.7 14.0 %collective-permute-start.3 = (f32[3,64]{1,0:T(4,128)S(1)}, f32[3,64]{1,0:T(4,128)S(1)}, u32[]{:S(2)}, u32[]{:S(2)}) collective-permute-start(f32[3,64]{1,0:T(4,128)S(1)} %get-tuple-element.39), channel_id=1, source_target_pairs={{16,0},{20,4},{24,8},{28,12},{17,1},{21,5},{25,9},{29,13},{18,2},{... | collective-permute-start | bytes 2312 | tf_op jit(solution)/shard_map/ppermute | solution.py:10
  4.0 12.7 %collective-permute-start.4 = (f32[3,64]{1,0:T(4,128)S(1)}, f32[3,64]{1,0:T(4,128)S(1)}, u32[]{:S(2)}, u32[]{:S(2)}) collective-permute-start(f32[3,64]{1,0:T(4,128)S(1)} %get-tuple-element.39), channel_id=1, source_target_pairs={{0,16},{4,20},{8,24},{12,28},{1,17},{5,21},{9,25},{13,29},{2,18},{... | collective-permute-start | bytes 2312 | tf_op jit(solution)/shard_map/ppermute | solution.py:10
  10.0 22.7 %collective-permute-start.2 = (f32[3,64,1]{2,1,0:T(8,128)S(1)}, f32[3,64,1]{2,1,0:T(8,128)S(1)}, u32[]{:S(2)}, u32[]{:S(2)}) collective-permute-start(f32[3,64,1]{2,1,0:T(8,128)S(1)} %get-tuple-element.41), channel_id=1, source_target_pairs={{1,0},{2,1},{3,2},{5,4},{6,5},{7,6},{9,8},{10,9},{11,10},{13,12},{... | collective-permute-start | bytes 2312 | tf_op jit(solution)/shard_map/ppermute | solution.py:23
  11.3 21.4 %collective-permute-start.9 = (f32[3,64,1]{2,1,0:T(8,128)S(1)}, f32[3,64,1]{2,1,0:T(8,128)S(1)}, u32[]{:S(2)}, u32[]{:S(2)}) collective-permute-start(f32[3,64,1]{2,1,0:T(8,128)S(1)} %get-tuple-element.40), channel_id=1, source_target_pairs={{0,1},{1,2},{2,3},{4,5},{5,6},{6,7},{8,9},{9,10},{10,11},{12,13},{... | collective-permute-start | bytes 2312 | tf_op jit(solution)/shard_map/ppermute | solution.py:21
  14.4 18.4 %collective-permute-start = (f32[3,1,256]{2,1,0:T(1,128)S(1)}, f32[3,1,256]{2,1,0:T(1,128)S(1)}, u32[]{:S(2)}, u32[]{:S(2)}) collective-permute-start(f32[3,1,256]{2,1,0:T(1,128)S(1)} %get-tuple-element.37), channel_id=1, source_target_pairs={{4,0},{8,4},{12,8},{16,12},{20,16},{24,20},{28,24},{0,28},{5,1},{9... | collective-permute-start | bytes 9224 | tf_op jit(solution)/shard_map/ppermute | solution.py:23
  25.2 6.6 %collective-permute-start.8 = (f32[3,64]{1,0:T(4,128)S(1)}, f32[3,64]{1,0:T(4,128)S(1)}, u32[]{:S(2)}, u32[]{:S(2)}) collective-permute-start(f32[3,64]{1,0:T(4,128)S(1)} %select_select_fusion.7), channel_id=1, source_target_pairs={{0,4},{4,8},{8,12},{12,16},{16,20},{20,24},{24,28},{1,5},{5,9},{9,... | collective-permute-start | bytes 2312 | tf_op jit(solution)/shard_map/ppermute | solution.py:10
  30.1 6.3 %collective-permute-start.1 = (f32[3,1,256]{2,1,0:T(1,128)S(1)}, f32[3,1,256]{2,1,0:T(1,128)S(1)}, u32[]{:S(2)}, u32[]{:S(2)}) collective-permute-start(f32[3,1,256]{2,1,0:T(1,128)S(1)} %get-tuple-element.38), channel_id=1, source_target_pairs={{0,4},{4,8},{8,12},{12,16},{16,20},{20,24},{24,28},{28,0},{1,5},{5... | collective-permute-start | bytes 9224 | tf_op jit(solution)/shard_map/ppermute | solution.py:21
  36.8 8.1 %collective-permute-start.13 = (f32[3,64]{1,0:T(4,128)S(1)}, f32[3,64]{1,0:T(4,128)S(1)}, u32[]{:S(2)}, u32[]{:S(2)}) collective-permute-start(f32[3,64]{1,0:T(4,128)S(1)} %get-tuple-element.32), channel_id=1, source_target_pairs={{16,0},{20,4},{24,8},{28,12},{17,1},{21,5},{25,9},{29,13},{18,2},{... | collective-permute-start | bytes 2312 | tf_op jit(solution)/shard_map/ppermute | solution.py:10
  38.1 6.8 %collective-permute-start.14 = (f32[3,64]{1,0:T(4,128)S(1)}, f32[3,64]{1,0:T(4,128)S(1)}, u32[]{:S(2)}, u32[]{:S(2)}) collective-permute-start(f32[3,64]{1,0:T(4,128)S(1)} %get-tuple-element.32), channel_id=1, source_target_pairs={{0,16},{4,20},{8,24},{12,28},{1,17},{5,21},{9,25},{13,29},{2,18},{... | collective-permute-start | bytes 2312 | tf_op jit(solution)/shard_map/ppermute | solution.py:10
  43.6 18.4 %collective-permute-start.19 = (f32[3,64,1]{2,1,0:T(8,128)S(1)}, f32[3,64,1]{2,1,0:T(8,128)S(1)}, u32[]{:S(2)}, u32[]{:S(2)}) collective-permute-start(f32[3,64,1]{2,1,0:T(8,128)S(1)} %get-tuple-element.33), channel_id=1, source_target_pairs={{0,1},{1,2},{2,3},{4,5},{5,6},{6,7},{8,9},{9,10},{10,11},{12,13},{... | collective-permute-start | bytes 2312 | tf_op jit(solution)/shard_map/ppermute | solution.py:21
  44.9 7.3 %collective-permute-start.15 = (f32[3,64]{1,0:T(4,128)S(1)}, f32[3,64]{1,0:T(4,128)S(1)}, u32[]{:S(2)}, u32[]{:S(2)}) collective-permute-start(f32[3,64]{1,0:T(4,128)S(1)} %select_select_fusion.5), channel_id=1, source_target_pairs={{8,0},{12,4},{16,8},{20,12},{24,16},{28,20},{9,1},{13,5},{17,9},{2... | collective-permute-start | bytes 2312 | tf_op jit(solution)/shard_map/ppermute | solution.py:10
  50.9 11.0 %collective-permute-start.12 = (f32[3,64,1]{2,1,0:T(8,128)S(1)}, f32[3,64,1]{2,1,0:T(8,128)S(1)}, u32[]{:S(2)}, u32[]{:S(2)}) collective-permute-start(f32[3,64,1]{2,1,0:T(8,128)S(1)} %get-tuple-element.34), channel_id=1, source_target_pairs={{1,0},{2,1},{3,2},{5,4},{6,5},{7,6},{9,8},{10,9},{11,10},{13,12},{... | collective-permute-start | bytes 2312 | tf_op jit(solution)/shard_map/ppermute | solution.py:23
  52.2 9.4 %collective-permute-start.17 = (f32[3,64]{1,0:T(4,128)S(1)}, f32[3,64]{1,0:T(4,128)S(1)}, u32[]{:S(2)}, u32[]{:S(2)}) collective-permute-start(f32[3,64]{1,0:T(4,128)S(1)} %select_select_fusion.4), channel_id=1, source_target_pairs={{4,0},{8,4},{12,8},{16,12},{20,16},{24,20},{28,24},{5,1},{9,5},{13... | collective-permute-start | bytes 2312 | tf_op jit(solution)/shard_map/ppermute | solution.py:10
  53.5 8.1 %collective-permute-start.18 = (f32[3,64]{1,0:T(4,128)S(1)}, f32[3,64]{1,0:T(4,128)S(1)}, u32[]{:S(2)}, u32[]{:S(2)}) collective-permute-start(f32[3,64]{1,0:T(4,128)S(1)} %select_select_fusion.4), channel_id=1, source_target_pairs={{0,4},{4,8},{8,12},{12,16},{16,20},{20,24},{24,28},{1,5},{5,9},{9,... | collective-permute-start | bytes 2312 | tf_op jit(solution)/shard_map/ppermute | solution.py:10
  61.6 6.3 %collective-permute-start.11 = (f32[3,1,256]{2,1,0:T(1,128)S(1)}, f32[3,1,256]{2,1,0:T(1,128)S(1)}, u32[]{:S(2)}, u32[]{:S(2)}) collective-permute-start(f32[3,1,256]{2,1,0:T(1,128)S(1)} %get-tuple-element.36), channel_id=1, source_target_pairs={{0,4},{4,8},{8,12},{12,16},{16,20},{20,24},{24,28},{28,0},{1,5},{5... | collective-permute-start | bytes 9224 | tf_op jit(solution)/shard_map/ppermute | solution.py:21
  115.0 6.8 %collective-permute-start.23 = (f32[3,64]{1,0:T(4,128)S(1)}, f32[3,64]{1,0:T(4,128)S(1)}, u32[]{:S(2)}, u32[]{:S(2)}) collective-permute-start(f32[3,64]{1,0:T(4,128)S(1)} %get-tuple-element.27), channel_id=1, source_target_pairs={{16,0},{20,4},{24,8},{28,12},{17,1},{21,5},{25,9},{29,13},{18,2},{... | collective-permute-start | bytes 2312 | tf_op jit(solution)/shard_map/ppermute | solution.py:10
  116.3 6.7 %collective-permute-start.24 = (f32[3,64]{1,0:T(4,128)S(1)}, f32[3,64]{1,0:T(4,128)S(1)}, u32[]{:S(2)}, u32[]{:S(2)}) collective-permute-start(f32[3,64]{1,0:T(4,128)S(1)} %get-tuple-element.27), channel_id=1, source_target_pairs={{0,16},{4,20},{8,24},{12,28},{1,17},{5,21},{9,25},{13,29},{2,18},{... | collective-permute-start | bytes 2312 | tf_op jit(solution)/shard_map/ppermute | solution.py:10
  123.1 6.7 %collective-permute-start.25 = (f32[3,64]{1,0:T(4,128)S(1)}, f32[3,64]{1,0:T(4,128)S(1)}, u32[]{:S(2)}, u32[]{:S(2)}) collective-permute-start(f32[3,64]{1,0:T(4,128)S(1)} %select_select_fusion.2), channel_id=1, source_target_pairs={{8,0},{12,4},{16,8},{20,12},{24,16},{28,20},{9,1},{13,5},{17,9},{2... | collective-permute-start | bytes 2312 | tf_op jit(solution)/shard_map/ppermute | solution.py:10
  124.3 6.7 %collective-permute-start.26 = (f32[3,64]{1,0:T(4,128)S(1)}, f32[3,64]{1,0:T(4,128)S(1)}, u32[]{:S(2)}, u32[]{:S(2)}) collective-permute-start(f32[3,64]{1,0:T(4,128)S(1)} %select_select_fusion.2), channel_id=1, source_target_pairs={{0,8},{4,12},{8,16},{12,20},{16,24},{20,28},{1,9},{5,13},{9,17},{1... | collective-permute-start | bytes 2312 | tf_op jit(solution)/shard_map/ppermute | solution.py:10
  131.0 13.4 %collective-permute-start.27 = (f32[3,64]{1,0:T(4,128)S(1)}, f32[3,64]{1,0:T(4,128)S(1)}, u32[]{:S(2)}, u32[]{:S(2)}) collective-permute-start(f32[3,64]{1,0:T(4,128)S(1)} %select_select_fusion.1), channel_id=1, source_target_pairs={{4,0},{8,4},{12,8},{16,12},{20,16},{24,20},{28,24},{5,1},{9,5},{13... | collective-permute-start | bytes 2312 | tf_op jit(solution)/shard_map/ppermute | solution.py:10
  132.3 12.3 %collective-permute-start.28 = (f32[3,64]{1,0:T(4,128)S(1)}, f32[3,64]{1,0:T(4,128)S(1)}, u32[]{:S(2)}, u32[]{:S(2)}) collective-permute-start(f32[3,64]{1,0:T(4,128)S(1)} %select_select_fusion.1), channel_id=1, source_target_pairs={{0,4},{4,8},{8,12},{12,16},{16,20},{20,24},{24,28},{1,5},{5,9},{9,... | collective-permute-start | bytes 2312 | tf_op jit(solution)/shard_map/ppermute | solution.py:10
  137.3 7.7 %collective-permute-start.22 = (f32[3,64,1]{2,1,0:T(8,128)S(1)}, f32[3,64,1]{2,1,0:T(8,128)S(1)}, u32[]{:S(2)}, u32[]{:S(2)}) collective-permute-start(f32[3,64,1]{2,1,0:T(8,128)S(1)} %get-tuple-element.29), channel_id=1, source_target_pairs={{1,0},{2,1},{3,2},{5,4},{6,5},{7,6},{9,8},{10,9},{11,10},{13,12},{... | collective-permute-start | bytes 2312 | tf_op jit(solution)/shard_map/ppermute | solution.py:23
  138.6 6.4 %collective-permute-start.29 = (f32[3,64,1]{2,1,0:T(8,128)S(1)}, f32[3,64,1]{2,1,0:T(8,128)S(1)}, u32[]{:S(2)}, u32[]{:S(2)}) collective-permute-start(f32[3,64,1]{2,1,0:T(8,128)S(1)} %get-tuple-element.28), channel_id=1, source_target_pairs={{0,1},{1,2},{2,3},{4,5},{5,6},{6,7},{8,9},{9,10},{10,11},{12,13},{... | collective-permute-start | bytes 2312 | tf_op jit(solution)/shard_map/ppermute | solution.py:21
  144.5 6.3 %collective-permute-start.21 = (f32[3,1,256]{2,1,0:T(1,128)S(1)}, f32[3,1,256]{2,1,0:T(1,128)S(1)}, u32[]{:S(2)}, u32[]{:S(2)}) collective-permute-start(f32[3,1,256]{2,1,0:T(1,128)S(1)} %get-tuple-element.31), channel_id=1, source_target_pairs={{0,4},{4,8},{8,12},{12,16},{16,20},{20,24},{24,28},{28,0},{1,5},{5... | collective-permute-start | bytes 9224 | tf_op jit(solution)/shard_map/ppermute | solution.py:21
  (15 other events, 64.8 us)
where the time goes:
time: 204 us; the launch traced here: 203 us
  starting transfers between devices  78.7 us (39%)
  blocking collectives  75.1 us (37%)
  waiting for transfers between devices  19.2 us (9%)
  between operations  12.9 us (6%)
  local copies, waits for them, and re-layouts  9.87 us (5%)
  other arithmetic  6.94 us (3%)
    psum x2, blocking collectives, merged(): return lax.psum(jnp.stack(values), ('gx', 'gy'))  75.1 us
    ppermute x18, starting transfers between devices, shifted(): return lax.ppermute(value, axis, pairs)  56.8 us
    ppermute x6, waiting for transfers between devices, extended(): lax.ppermute(tail, axis, [(i, (i + 1) % count) for i in range(ends)])  13.2 us
    ppermute x6, starting transfers between devices, extended(): lax.ppermute(head, axis, [((i + 1) % count, i) for i in range(ends)])  12.6 us
    ppermute x6, starting transfers between devices, extended(): lax.ppermute(tail, axis, [(i, (i + 1) % count) for i in range(ends)])  9.27 us
    another operation x2, local copies, waits for them, and re-layouts, merged(): return lax.psum(jnp.stack(values), ('gx', 'gy'))  6.33 us
  transfers between devices with their start and end apart: 30, of which 8 were waited for; matrix products, arithmetic and copies ran while one was open for 1% of the time, Pallas kernels for 0%

commit v1 on v0

--- a/solution.py
+++ b/solution.py
@@ -101,7 +101,7 @@
     z0 = pre[2]
 
     def merged(values):
-        return lax.psum(jnp.stack(values), ("gx", "gy"))
+        return lax.psum(lax.psum(jnp.stack(values), "gy"), "gx")
 
     sums = merged(
         [inner(r, r), inner(w_scaled, r), inner(w_scaled, w_scaled), inner(ro, z0), inner(z0, az0)]

time: 204 us -> 175 us (0.86)
  blocking collectives: 75.1 us -> 46 us
    psum x2 -> x4, blocking collectives: 75.1 us -> 46 us  [merged(): return lax.psum(lax.psum(jnp.stack(values), 'gy'), 'gx')]
where the time goes in v1:
time: 175 us; the launch traced here: 174 us
  starting transfers between devices  78.3 us (45%)
  blocking collectives  46 us (26%)
  waiting for transfers between devices  19.4 us (11%)
  between operations  13.2 us (8%)
  local copies, waits for them, and re-layouts  9.92 us (6%)
  other arithmetic  7 us (4%)
    ppermute x18, starting transfers between devices, shifted(): return lax.ppermute(value, axis, pairs)  55.7 us
    psum x4, blocking collectives, merged(): return lax.psum(lax.psum(jnp.stack(values), 'gy'), 'gx')  46 us
    ppermute x6, waiting for transfers between devices, extended(): lax.ppermute(tail, axis, [(i, (i + 1) % count) for i in range(ends)])  13.6 us
    ppermute x6, starting transfers between devices, extended(): lax.ppermute(head, axis, [((i + 1) % count, i) for i in range(ends)])  13.5 us
    ppermute x6, starting transfers between devices, extended(): lax.ppermute(tail, axis, [(i, (i + 1) % count) for i in range(ends)])  9.1 us
    another operation x2, local copies, waits for them, and re-layouts, merged(): return lax.psum(lax.psum(jnp.stack(values), 'gy'), 'gx')  6.44 us
    ppermute x18, waiting for transfers between devices, shifted(): return lax.ppermute(value, axis, pairs)  3.84 us
  transfers between devices with their start and end apart: 30, of which 8 were waited for; matrix products, arithmetic and copies ran while one was open for 1% of the time, Pallas kernels for 0%

profile of v1, /device:TPU:0, one launch (start us, length us, event | category | flops | bytes accessed | tf_op | source)
XLA Modules:
  0.0 173.8 jit_solution(11186975708651564393)
XLA Ops:
  4.0 6.0 %collective-permute-start.4 = (f32[3,64]{1,0:T(4,128)S(1)}, f32[3,64]{1,0:T(4,128)S(1)}, u32[]{:S(2)}, u32[]{:S(2)}) collective-permute-start(f32[3,64]{1,0:T(4,128)S(1)} %get-tuple-element.39), channel_id=1, source_target_pairs={{0,16},{4,20},{8,24},{12,28},{1,17},{5,21},{9,25},{13,29},{2,18},{... | collective-permute-start | bytes 2312 | tf_op jit(solution)/shard_map/ppermute | solution.py:10
  11.3 3.0 %collective-permute-start.9 = (f32[3,64,1]{2,1,0:T(8,128)S(1)}, f32[3,64,1]{2,1,0:T(8,128)S(1)}, u32[]{:S(2)}, u32[]{:S(2)}) collective-permute-start(f32[3,64,1]{2,1,0:T(8,128)S(1)} %get-tuple-element.40), channel_id=1, source_target_pairs={{0,1},{1,2},{2,3},{4,5},{5,6},{6,7},{8,9},{9,10},{10,11},{12,13},{... | collective-permute-start | bytes 2312 | tf_op jit(solution)/shard_map/ppermute | solution.py:21
  14.4 2.4 %collective-permute-start = (f32[3,1,256]{2,1,0:T(1,128)S(1)}, f32[3,1,256]{2,1,0:T(1,128)S(1)}, u32[]{:S(2)}, u32[]{:S(2)}) collective-permute-start(f32[3,1,256]{2,1,0:T(1,128)S(1)} %get-tuple-element.37), channel_id=1, source_target_pairs={{4,0},{8,4},{12,8},{16,12},{20,16},{24,20},{28,24},{0,28},{5,1},{9... | collective-permute-start | bytes 9224 | tf_op jit(solution)/shard_map/ppermute | solution.py:23
  18.1 4.5 %collective-permute-start.6 = (f32[3,64]{1,0:T(4,128)S(1)}, f32[3,64]{1,0:T(4,128)S(1)}, u32[]{:S(2)}, u32[]{:S(2)}) collective-permute-start(f32[3,64]{1,0:T(4,128)S(1)} %select_select_fusion.8), channel_id=1, source_target_pairs={{0,8},{4,12},{8,16},{12,20},{16,24},{20,28},{1,9},{5,13},{9,17},{1... | collective-permute-start | bytes 2312 | tf_op jit(solution)/shard_map/ppermute | solution.py:10
  25.2 4.5 %collective-permute-start.8 = (f32[3,64]{1,0:T(4,128)S(1)}, f32[3,64]{1,0:T(4,128)S(1)}, u32[]{:S(2)}, u32[]{:S(2)}) collective-permute-start(f32[3,64]{1,0:T(4,128)S(1)} %select_select_fusion.7), channel_id=1, source_target_pairs={{0,4},{4,8},{8,12},{12,16},{16,20},{20,24},{24,28},{1,5},{5,9},{9,... | collective-permute-start | bytes 2312 | tf_op jit(solution)/shard_map/ppermute | solution.py:10
  30.1 1.7 collective-permute-start.1
  32.7 3.6 %collective-permute-done.1 = f32[3,1,256]{2,1,0:T(1,128)S(1)} collective-permute-done((f32[3,1,256]{2,1,0:T(1,128)S(1)}, f32[3,1,256]{2,1,0:T(1,128)S(1)}, u32[]{:S(2)}, u32[]{:S(2)}) %collective-permute-start.1) | collective-permute-done | bytes 3104 | tf_op jit(solution)/shard_map/ppermute | solution.py:21
  38.1 5.4 %collective-permute-start.14 = (f32[3,64]{1,0:T(4,128)S(1)}, f32[3,64]{1,0:T(4,128)S(1)}, u32[]{:S(2)}, u32[]{:S(2)}) collective-permute-start(f32[3,64]{1,0:T(4,128)S(1)} %get-tuple-element.32), channel_id=1, source_target_pairs={{0,16},{4,20},{8,24},{12,28},{1,17},{5,21},{9,25},{13,29},{2,18},{... | collective-permute-start | bytes 2312 | tf_op jit(solution)/shard_map/ppermute | solution.py:10
  46.2 4.5 %collective-permute-start.16 = (f32[3,64]{1,0:T(4,128)S(1)}, f32[3,64]{1,0:T(4,128)S(1)}, u32[]{:S(2)}, u32[]{:S(2)}) collective-permute-start(f32[3,64]{1,0:T(4,128)S(1)} %select_select_fusion.5), channel_id=1, source_target_pairs={{0,8},{4,12},{8,16},{12,20},{16,24},{20,28},{1,9},{5,13},{9,17},{1... | collective-permute-start | bytes 2312 | tf_op jit(solution)/shard_map/ppermute | solution.py:10
  53.5 4.5 %collective-permute-start.18 = (f32[3,64]{1,0:T(4,128)S(1)}, f32[3,64]{1,0:T(4,128)S(1)}, u32[]{:S(2)}, u32[]{:S(2)}) collective-permute-start(f32[3,64]{1,0:T(4,128)S(1)} %select_select_fusion.4), channel_id=1, source_target_pairs={{0,4},{4,8},{8,12},{12,16},{16,20},{20,24},{24,28},{1,5},{5,9},{9,... | collective-permute-start | bytes 2312 | tf_op jit(solution)/shard_map/ppermute | solution.py:10
  58.1 3.5 %collective-permute-start.10 = (f32[3,1,256]{2,1,0:T(1,128)S(1)}, f32[3,1,256]{2,1,0:T(1,128)S(1)}, u32[]{:S(2)}, u32[]{:S(2)}) collective-permute-start(f32[3,1,256]{2,1,0:T(1,128)S(1)} %get-tuple-element.35), channel_id=1, source_target_pairs={{4,0},{8,4},{12,8},{16,12},{20,16},{24,20},{28,24},{0,28},{5,1},{9... | collective-permute-start | bytes 9224 | tf_op jit(solution)/shard_map/ppermute | solution.py:23
  62.9 5.0 %collective-permute-done.11 = f32[3,1,256]{2,1,0:T(1,128)S(1)} collective-permute-done((f32[3,1,256]{2,1,0:T(1,128)S(1)}, f32[3,1,256]{2,1,0:T(1,128)S(1)}, u32[]{:S(2)}, u32[]{:S(2)}) %collective-permute-start.11) | collective-permute-done | bytes 3104 | tf_op jit(solution)/shard_map/ppermute | solution.py:21
  69.5 3.2 %stack.109 = f32[5]{0:T(128)S(1)} concatenate(f32[1]{0:T(128)} %bitcast.17, f32[1]{0:T(128)} %bitcast.18, f32[1]{0:T(128)} %bitcast.19, f32[1]{0:T(128)} %bitcast.22, f32[1]{0:T(128)} %bitcast.24), dimensions={0} | concatenate | bytes 40 | tf_op jit(solution)/shard_map/stack | solution.py:104
  72.7 5.6 %psum.28 = f32[5]{0:T(128)S(1)} all-reduce(f32[5]{0:T(128)S(1)} %stack.109), channel_id=1, replica_groups=mesh['gx'=8,'gy'=4] {'gy'}, use_global_device_ids=true, to_apply=%region_5.6 | all-reduce | flops 5 | bytes 40 | tf_op jit(solution)/shard_map/psum | solution.py:104
  78.3 17.1 %psum.29 = f32[5]{0:T(128)S(1)} all-reduce(f32[5]{0:T(128)S(1)} %psum.28), channel_id=1, replica_groups=mesh['gx'=8,'gy'=4] {'gx'}, use_global_device_ids=true, to_apply=%region_6.7 | all-reduce | flops 5 | bytes 40 | tf_op jit(solution)/shard_map/psum | solution.py:104
  102.3 5.4 %collective-permute-start.24 = (f32[3,64]{1,0:T(4,128)S(1)}, f32[3,64]{1,0:T(4,128)S(1)}, u32[]{:S(2)}, u32[]{:S(2)}) collective-permute-start(f32[3,64]{1,0:T(4,128)S(1)} %get-tuple-element.27), channel_id=1, source_target_pairs={{0,16},{4,20},{8,24},{12,28},{1,17},{5,21},{9,25},{13,29},{2,18},{... | collective-permute-start | bytes 2312 | tf_op jit(solution)/shard_map/ppermute | solution.py:10
  110.3 4.5 %collective-permute-start.26 = (f32[3,64]{1,0:T(4,128)S(1)}, f32[3,64]{1,0:T(4,128)S(1)}, u32[]{:S(2)}, u32[]{:S(2)}) collective-permute-start(f32[3,64]{1,0:T(4,128)S(1)} %select_select_fusion.2), channel_id=1, source_target_pairs={{0,8},{4,12},{8,16},{12,20},{16,24},{20,28},{1,9},{5,13},{9,17},{1... | collective-permute-start | bytes 2312 | tf_op jit(solution)/shard_map/ppermute | solution.py:10
  117.5 4.5 %collective-permute-start.28 = (f32[3,64]{1,0:T(4,128)S(1)}, f32[3,64]{1,0:T(4,128)S(1)}, u32[]{:S(2)}, u32[]{:S(2)}) collective-permute-start(f32[3,64]{1,0:T(4,128)S(1)} %select_select_fusion.1), channel_id=1, source_target_pairs={{0,4},{4,8},{8,12},{12,16},{16,20},{20,24},{24,28},{1,5},{5,9},{9,... | collective-permute-start | bytes 2312 | tf_op jit(solution)/shard_map/ppermute | solution.py:10
  123.4 3.0 %collective-permute-start.29 = (f32[3,64,1]{2,1,0:T(8,128)S(1)}, f32[3,64,1]{2,1,0:T(8,128)S(1)}, u32[]{:S(2)}, u32[]{:S(2)}) collective-permute-start(f32[3,64,1]{2,1,0:T(8,128)S(1)} %get-tuple-element.28), channel_id=1, source_target_pairs={{0,1},{1,2},{2,3},{4,5},{5,6},{6,7},{8,9},{9,10},{10,11},{12,13},{... | collective-permute-start | bytes 2312 | tf_op jit(solution)/shard_map/ppermute | solution.py:21
  126.5 3.8 %collective-permute-start.20 = (f32[3,1,256]{2,1,0:T(1,128)S(1)}, f32[3,1,256]{2,1,0:T(1,128)S(1)}, u32[]{:S(2)}, u32[]{:S(2)}) collective-permute-start(f32[3,1,256]{2,1,0:T(1,128)S(1)} %get-tuple-element.30), channel_id=1, source_target_pairs={{4,0},{8,4},{12,8},{16,12},{20,16},{24,20},{28,24},{0,28},{5,1},{9... | collective-permute-start | bytes 9224 | tf_op jit(solution)/shard_map/ppermute | solution.py:23
  131.6 5.0 %collective-permute-done.21 = f32[3,1,256]{2,1,0:T(1,128)S(1)} collective-permute-done((f32[3,1,256]{2,1,0:T(1,128)S(1)}, f32[3,1,256]{2,1,0:T(1,128)S(1)}, u32[]{:S(2)}, u32[]{:S(2)}) %collective-permute-start.21) | collective-permute-done | bytes 3104 | tf_op jit(solution)/shard_map/ppermute | solution.py:21
  138.1 3.2 %stack.118 = f32[5]{0:T(128)S(1)} concatenate(f32[1]{0:T(128)} %bitcast.35, f32[1]{0:T(128)} %bitcast.36, f32[1]{0:T(128)} %bitcast.37, f32[1]{0:T(128)} %bitcast.39, f32[1]{0:T(128)} %bitcast.41), dimensions={0} | concatenate | bytes 40 | tf_op jit(solution)/shard_map/stack | solution.py:104
  141.3 5.7 %psum.30 = f32[5]{0:T(128)S(1)} all-reduce(f32[5]{0:T(128)S(1)} %stack.118), channel_id=1, replica_groups=mesh['gx'=8,'gy'=4] {'gy'}, use_global_device_ids=true, to_apply=%region_12.13 | all-reduce | flops 5 | bytes 40 | tf_op jit(solution)/shard_map/psum | solution.py:104
  147.1 17.5 %psum.31 = f32[5]{0:T(128)S(1)} all-reduce(f32[5]{0:T(128)S(1)} %psum.30), channel_id=1, replica_groups=mesh['gx'=8,'gy'=4] {'gx'}, use_global_device_ids=true, to_apply=%region_13.14 | all-reduce | flops 5 | bytes 40 | tf_op jit(solution)/shard_map/psum | solution.py:104
  (112 shorter events, 33.0 us)
Async XLA Ops:
  2.7 14.0 %collective-permute-start.3 = (f32[3,64]{1,0:T(4,128)S(1)}, f32[3,64]{1,0:T(4,128)S(1)}, u32[]{:S(2)}, u32[]{:S(2)}) collective-permute-start(f32[3,64]{1,0:T(4,128)S(1)} %get-tuple-element.39), channel_id=1, source_target_pairs={{16,0},{20,4},{24,8},{28,12},{17,1},{21,5},{25,9},{29,13},{18,2},{... | collective-permute-start | bytes 2312 | tf_op jit(solution)/shard_map/ppermute | solution.py:10
  4.0 12.7 %collective-permute-start.4 = (f32[3,64]{1,0:T(4,128)S(1)}, f32[3,64]{1,0:T(4,128)S(1)}, u32[]{:S(2)}, u32[]{:S(2)}) collective-permute-start(f32[3,64]{1,0:T(4,128)S(1)} %get-tuple-element.39), channel_id=1, source_target_pairs={{0,16},{4,20},{8,24},{12,28},{1,17},{5,21},{9,25},{13,29},{2,18},{... | collective-permute-start | bytes 2312 | tf_op jit(solution)/shard_map/ppermute | solution.py:10
  10.0 22.7 %collective-permute-start.2 = (f32[3,64,1]{2,1,0:T(8,128)S(1)}, f32[3,64,1]{2,1,0:T(8,128)S(1)}, u32[]{:S(2)}, u32[]{:S(2)}) collective-permute-start(f32[3,64,1]{2,1,0:T(8,128)S(1)} %get-tuple-element.41), channel_id=1, source_target_pairs={{1,0},{2,1},{3,2},{5,4},{6,5},{7,6},{9,8},{10,9},{11,10},{13,12},{... | collective-permute-start | bytes 2312 | tf_op jit(solution)/shard_map/ppermute | solution.py:23
  11.3 21.4 %collective-permute-start.9 = (f32[3,64,1]{2,1,0:T(8,128)S(1)}, f32[3,64,1]{2,1,0:T(8,128)S(1)}, u32[]{:S(2)}, u32[]{:S(2)}) collective-permute-start(f32[3,64,1]{2,1,0:T(8,128)S(1)} %get-tuple-element.40), channel_id=1, source_target_pairs={{0,1},{1,2},{2,3},{4,5},{5,6},{6,7},{8,9},{9,10},{10,11},{12,13},{... | collective-permute-start | bytes 2312 | tf_op jit(solution)/shard_map/ppermute | solution.py:21
  14.4 18.4 %collective-permute-start = (f32[3,1,256]{2,1,0:T(1,128)S(1)}, f32[3,1,256]{2,1,0:T(1,128)S(1)}, u32[]{:S(2)}, u32[]{:S(2)}) collective-permute-start(f32[3,1,256]{2,1,0:T(1,128)S(1)} %get-tuple-element.37), channel_id=1, source_target_pairs={{4,0},{8,4},{12,8},{16,12},{20,16},{24,20},{28,24},{0,28},{5,1},{9... | collective-permute-start | bytes 9224 | tf_op jit(solution)/shard_map/ppermute | solution.py:23
  24.0 6.1 %collective-permute-start.7 = (f32[3,64]{1,0:T(4,128)S(1)}, f32[3,64]{1,0:T(4,128)S(1)}, u32[]{:S(2)}, u32[]{:S(2)}) collective-permute-start(f32[3,64]{1,0:T(4,128)S(1)} %select_select_fusion.7), channel_id=1, source_target_pairs={{4,0},{8,4},{12,8},{16,12},{20,16},{24,20},{28,24},{5,1},{9,5},{13... | collective-permute-start | bytes 2312 | tf_op jit(solution)/shard_map/ppermute | solution.py:10
  25.2 6.6 %collective-permute-start.8 = (f32[3,64]{1,0:T(4,128)S(1)}, f32[3,64]{1,0:T(4,128)S(1)}, u32[]{:S(2)}, u32[]{:S(2)}) collective-permute-start(f32[3,64]{1,0:T(4,128)S(1)} %select_select_fusion.7), channel_id=1, source_target_pairs={{0,4},{4,8},{8,12},{12,16},{16,20},{20,24},{24,28},{1,5},{5,9},{9,... | collective-permute-start | bytes 2312 | tf_op jit(solution)/shard_map/ppermute | solution.py:10
  30.1 6.3 %collective-permute-start.1 = (f32[3,1,256]{2,1,0:T(1,128)S(1)}, f32[3,1,256]{2,1,0:T(1,128)S(1)}, u32[]{:S(2)}, u32[]{:S(2)}) collective-permute-start(f32[3,1,256]{2,1,0:T(1,128)S(1)} %get-tuple-element.38), channel_id=1, source_target_pairs={{0,4},{4,8},{8,12},{12,16},{16,20},{20,24},{24,28},{28,0},{1,5},{5... | collective-permute-start | bytes 9224 | tf_op jit(solution)/shard_map/ppermute | solution.py:21
  36.8 8.1 %collective-permute-start.13 = (f32[3,64]{1,0:T(4,128)S(1)}, f32[3,64]{1,0:T(4,128)S(1)}, u32[]{:S(2)}, u32[]{:S(2)}) collective-permute-start(f32[3,64]{1,0:T(4,128)S(1)} %get-tuple-element.32), channel_id=1, source_target_pairs={{16,0},{20,4},{24,8},{28,12},{17,1},{21,5},{25,9},{29,13},{18,2},{... | collective-permute-start | bytes 2312 | tf_op jit(solution)/shard_map/ppermute | solution.py:10
  38.1 6.8 %collective-permute-start.14 = (f32[3,64]{1,0:T(4,128)S(1)}, f32[3,64]{1,0:T(4,128)S(1)}, u32[]{:S(2)}, u32[]{:S(2)}) collective-permute-start(f32[3,64]{1,0:T(4,128)S(1)} %get-tuple-element.32), channel_id=1, source_target_pairs={{0,16},{4,20},{8,24},{12,28},{1,17},{5,21},{9,25},{13,29},{2,18},{... | collective-permute-start | bytes 2312 | tf_op jit(solution)/shard_map/ppermute | solution.py:10
  43.6 18.4 %collective-permute-start.19 = (f32[3,64,1]{2,1,0:T(8,128)S(1)}, f32[3,64,1]{2,1,0:T(8,128)S(1)}, u32[]{:S(2)}, u32[]{:S(2)}) collective-permute-start(f32[3,64,1]{2,1,0:T(8,128)S(1)} %get-tuple-element.33), channel_id=1, source_target_pairs={{0,1},{1,2},{2,3},{4,5},{5,6},{6,7},{8,9},{9,10},{10,11},{12,13},{... | collective-permute-start | bytes 2312 | tf_op jit(solution)/shard_map/ppermute | solution.py:21
  44.9 7.3 %collective-permute-start.15 = (f32[3,64]{1,0:T(4,128)S(1)}, f32[3,64]{1,0:T(4,128)S(1)}, u32[]{:S(2)}, u32[]{:S(2)}) collective-permute-start(f32[3,64]{1,0:T(4,128)S(1)} %select_select_fusion.5), channel_id=1, source_target_pairs={{8,0},{12,4},{16,8},{20,12},{24,16},{28,20},{9,1},{13,5},{17,9},{2... | collective-permute-start | bytes 2312 | tf_op jit(solution)/shard_map/ppermute | solution.py:10
  46.2 6.0 %collective-permute-start.16 = (f32[3,64]{1,0:T(4,128)S(1)}, f32[3,64]{1,0:T(4,128)S(1)}, u32[]{:S(2)}, u32[]{:S(2)}) collective-permute-start(f32[3,64]{1,0:T(4,128)S(1)} %select_select_fusion.5), channel_id=1, source_target_pairs={{0,8},{4,12},{8,16},{12,20},{16,24},{20,28},{1,9},{5,13},{9,17},{1... | collective-permute-start | bytes 2312 | tf_op jit(solution)/shard_map/ppermute | solution.py:10
  50.9 11.0 %collective-permute-start.12 = (f32[3,64,1]{2,1,0:T(8,128)S(1)}, f32[3,64,1]{2,1,0:T(8,128)S(1)}, u32[]{:S(2)}, u32[]{:S(2)}) collective-permute-start(f32[3,64,1]{2,1,0:T(8,128)S(1)} %get-tuple-element.34), channel_id=1, source_target_pairs={{1,0},{2,1},{3,2},{5,4},{6,5},{7,6},{9,8},{10,9},{11,10},{13,12},{... | collective-permute-start | bytes 2312 | tf_op jit(solution)/shard_map/ppermute | solution.py:23
  52.2 9.4 %collective-permute-start.17 = (f32[3,64]{1,0:T(4,128)S(1)}, f32[3,64]{1,0:T(4,128)S(1)}, u32[]{:S(2)}, u32[]{:S(2)}) collective-permute-start(f32[3,64]{1,0:T(4,128)S(1)} %select_select_fusion.4), channel_id=1, source_target_pairs={{4,0},{8,4},{12,8},{16,12},{20,16},{24,20},{28,24},{5,1},{9,5},{13... | collective-permute-start | bytes 2312 | tf_op jit(solution)/shard_map/ppermute | solution.py:10
  53.5 8.1 %collective-permute-start.18 = (f32[3,64]{1,0:T(4,128)S(1)}, f32[3,64]{1,0:T(4,128)S(1)}, u32[]{:S(2)}, u32[]{:S(2)}) collective-permute-start(f32[3,64]{1,0:T(4,128)S(1)} %select_select_fusion.4), channel_id=1, source_target_pairs={{0,4},{4,8},{8,12},{12,16},{16,20},{20,24},{24,28},{1,5},{5,9},{9,... | collective-permute-start | bytes 2312 | tf_op jit(solution)/shard_map/ppermute | solution.py:10
  61.6 6.3 %collective-permute-start.11 = (f32[3,1,256]{2,1,0:T(1,128)S(1)}, f32[3,1,256]{2,1,0:T(1,128)S(1)}, u32[]{:S(2)}, u32[]{:S(2)}) collective-permute-start(f32[3,1,256]{2,1,0:T(1,128)S(1)} %get-tuple-element.36), channel_id=1, source_target_pairs={{0,4},{4,8},{8,12},{12,16},{16,20},{20,24},{24,28},{28,0},{1,5},{5... | collective-permute-start | bytes 9224 | tf_op jit(solution)/shard_map/ppermute | solution.py:21
  101.0 6.8 %collective-permute-start.23 = (f32[3,64]{1,0:T(4,128)S(1)}, f32[3,64]{1,0:T(4,128)S(1)}, u32[]{:S(2)}, u32[]{:S(2)}) collective-permute-start(f32[3,64]{1,0:T(4,128)S(1)} %get-tuple-element.27), channel_id=1, source_target_pairs={{16,0},{20,4},{24,8},{28,12},{17,1},{21,5},{25,9},{29,13},{18,2},{... | collective-permute-start | bytes 2312 | tf_op jit(solution)/shard_map/ppermute | solution.py:10
  102.3 6.7 %collective-permute-start.24 = (f32[3,64]{1,0:T(4,128)S(1)}, f32[3,64]{1,0:T(4,128)S(1)}, u32[]{:S(2)}, u32[]{:S(2)}) collective-permute-start(f32[3,64]{1,0:T(4,128)S(1)} %get-tuple-element.27), channel_id=1, source_target_pairs={{0,16},{4,20},{8,24},{12,28},{1,17},{5,21},{9,25},{13,29},{2,18},{... | collective-permute-start | bytes 2312 | tf_op jit(solution)/shard_map/ppermute | solution.py:10
  116.2 14.1 %collective-permute-start.27 = (f32[3,64]{1,0:T(4,128)S(1)}, f32[3,64]{1,0:T(4,128)S(1)}, u32[]{:S(2)}, u32[]{:S(2)}) collective-permute-start(f32[3,64]{1,0:T(4,128)S(1)} %select_select_fusion.1), channel_id=1, source_target_pairs={{4,0},{8,4},{12,8},{16,12},{20,16},{24,20},{28,24},{5,1},{9,5},{13... | collective-permute-start | bytes 2312 | tf_op jit(solution)/shard_map/ppermute | solution.py:10
  117.5 12.8 %collective-permute-start.28 = (f32[3,64]{1,0:T(4,128)S(1)}, f32[3,64]{1,0:T(4,128)S(1)}, u32[]{:S(2)}, u32[]{:S(2)}) collective-permute-start(f32[3,64]{1,0:T(4,128)S(1)} %select_select_fusion.1), channel_id=1, source_target_pairs={{0,4},{4,8},{8,12},{12,16},{16,20},{20,24},{24,28},{1,5},{5,9},{9,... | collective-permute-start | bytes 2312 | tf_op jit(solution)/shard_map/ppermute | solution.py:10
  122.1 8.4 %collective-permute-start.22 = (f32[3,64,1]{2,1,0:T(8,128)S(1)}, f32[3,64,1]{2,1,0:T(8,128)S(1)}, u32[]{:S(2)}, u32[]{:S(2)}) collective-permute-start(f32[3,64,1]{2,1,0:T(8,128)S(1)} %get-tuple-element.29), channel_id=1, source_target_pairs={{1,0},{2,1},{3,2},{5,4},{6,5},{7,6},{9,8},{10,9},{11,10},{13,12},{... | collective-permute-start | bytes 2312 | tf_op jit(solution)/shard_map/ppermute | solution.py:23
  123.4 7.1 %collective-permute-start.29 = (f32[3,64,1]{2,1,0:T(8,128)S(1)}, f32[3,64,1]{2,1,0:T(8,128)S(1)}, u32[]{:S(2)}, u32[]{:S(2)}) collective-permute-start(f32[3,64,1]{2,1,0:T(8,128)S(1)} %get-tuple-element.28), channel_id=1, source_target_pairs={{0,1},{1,2},{2,3},{4,5},{5,6},{6,7},{8,9},{9,10},{10,11},{12,13},{... | collective-permute-start | bytes 2312 | tf_op jit(solution)/shard_map/ppermute | solution.py:21
  130.2 6.3 %collective-permute-start.21 = (f32[3,1,256]{2,1,0:T(1,128)S(1)}, f32[3,1,256]{2,1,0:T(1,128)S(1)}, u32[]{:S(2)}, u32[]{:S(2)}) collective-permute-start(f32[3,1,256]{2,1,0:T(1,128)S(1)} %get-tuple-element.31), channel_id=1, source_target_pairs={{0,4},{4,8},{8,12},{12,16},{16,20},{20,24},{24,28},{28,0},{1,5},{5... | collective-permute-start | bytes 9224 | tf_op jit(solution)/shard_map/ppermute | solution.py:21
  (15 other events, 64.9 us)
